TPU v7x, 32 devices: a whole 2x2x4 slice. The times are simulated.
32 devices in a mesh: tm: 16 (over z, y, x), rows: 2 (over core).
Axes of the slice: x: 2, y: 2, z: 4, core: 2. Of those that a mesh axis runs over, the one named last changes fastest.
Arguments:
- resid: float32 [2, 16, 16, 512], P(None, 'tm', 'rows'), may hold values from -3 to 3
- basis: float32 [4, 2, 16, 16, 512], P(None, None, 'tm', 'rows'), may hold values from -0.01171875 to 0.01171875
Outputs:
- precond: float32 [2, 16, 16, 512], P(None, 'tm', 'rows')
- image: float32 [2, 16, 16, 512], P(None, 'tm', 'rows')
- gram: float32 [5], replicated
All inputs are finite; a program needn't handle non-finite values.
Results may differ from a plain program's by a relative error of at most 0.0005.
Values sent between devices are 32-bit elements; how exact they have to be, the bound alone decides.
A program may use at most 64 MiB of HBM per device.

v0:
```python
import math
import jax
import jax.numpy as jnp
from jax import lax
from jax.sharding import PartitionSpec as P

SWEEPS = 4
ALPHA = 0.01


def padded_2(shard, sides, width):
    for axis, dim in sides:
        count, length = (lax.axis_size(axis), shard.shape[dim])
        up = [(i, (i + 1) % count) for i in range(count - 1)]
        down = [(j, i) for i, j in up]
        last = lax.slice_in_dim(shard, length - width, length, axis=dim)
        first = lax.slice_in_dim(shard, 0, width, axis=dim)
        before = lax.ppermute(last, axis, up)
        after = lax.ppermute(first, axis, down)
        shard = jnp.concatenate([before, shard, after], axis=dim)
    return shard


def shifted(value, axis, steps):
    count = lax.axis_size(axis)
    first, last = (max(0, -steps), min(count, count - steps))
    return lax.ppermute(value, axis, [(source, source + steps) for source in range(first, last)])


def neighbours(padded):
    middle = padded[:, 1:-1]
    sides = jnp.pad(middle, ((0, 0), (0, 0), (1, 1)))
    return padded[:, 2:] + padded[:, :-2] + sides[:, :, 2:] + sides[:, :, :-2]


def cmul(left, right_re, right_im):
    return jnp.stack(
        [left[0] * right_re - left[1] * right_im, left[0] * right_im + left[1] * right_re]
    )


def phases(first, second, steps):
    turns = first * second % steps
    angle = turns.astype(jnp.float32) * (2.0 * math.pi / steps)
    return (jnp.cos(angle), jnp.sin(angle))


def on_device(resid, basis):
    steps = lax.axis_size("tm")
    coupling = 16.0 / (steps * steps)
    me = lax.axis_index("tm")
    rows_dev = resid.shape[2]
    cols = resid.shape[3]
    cells = rows_dev * cols
    piece = cells // steps
    mine = me.astype(jnp.float32)
    gamma = jnp.power(jnp.float32(ALPHA), mine / steps)
    scaled = resid[:, 0] * gamma
    ordinal = jnp.arange(steps, dtype=jnp.int32)
    cos_table, sin_table = phases(ordinal[:, None], ordinal[None, :], steps)
    blocks = lax.all_to_all(
        scaled.reshape(1, 2, cells), "tm", split_axis=2, concat_axis=0, tiled=True
    )
    flat = blocks.reshape(steps, 2 * piece)
    real_part = jnp.dot(cos_table, flat, precision=lax.Precision.HIGHEST)
    imag_part = -jnp.dot(sin_table, flat, precision=lax.Precision.HIGHEST)
    stacked = jnp.stack([real_part, imag_part], 1).reshape(steps, 2, 2, piece)
    spectrum = lax.all_to_all(stacked, "tm", split_axis=0, concat_axis=3, tiled=True)
    rhat = spectrum[0].reshape(2, 2, rows_dev, cols)
    base = jnp.power(jnp.float32(ALPHA), jnp.float32(1.0) / steps)
    angle = mine * (2.0 * math.pi / steps)
    lam_re = 1.0 - base * jnp.cos(angle)
    lam_im = base * jnp.sin(angle)
    disp_spec = rhat[:, 0]
    right = cmul(disp_spec, lam_re, lam_im) + rhat[:, 1]
    den_re = lam_re * lam_re - lam_im * lam_im + 4.0 * coupling
    den_im = 2.0 * lam_re * lam_im
    magnitude = den_re * den_re + den_im * den_im
    inv_re = den_re / magnitude
    inv_im = -den_im / magnitude
    uhat = cmul(right, inv_re, inv_im)
    for sweep in range(SWEEPS - 1):
        padded = padded_2(uhat, (("rows", 1),), 1)
        uhat = cmul(right + coupling * neighbours(padded), inv_re, inv_im)
    vhat = cmul(uhat, lam_re, lam_im) - disp_spec
    yhat = jnp.stack([uhat, vhat], 1)
    spread = lax.all_to_all(
        yhat.reshape(1, 2, 2, cells), "tm", split_axis=3, concat_axis=0, tiled=True
    )
    real_rows = spread[:, 0].reshape(steps, 2 * piece)
    imag_rows = spread[:, 1].reshape(steps, 2 * piece)
    undo = jnp.power(jnp.float32(ALPHA), -ordinal.astype(jnp.float32) / steps) / steps
    history = jnp.dot(cos_table, real_rows, precision=lax.Precision.HIGHEST) - jnp.dot(
        sin_table, imag_rows, precision=lax.Precision.HIGHEST
    )
    history = (history * undo[:, None]).reshape(steps, 2, piece)
    returned = lax.all_to_all(history, "tm", split_axis=0, concat_axis=2, tiled=True)
    precond = returned[0].reshape(2, rows_dev, cols)
    earlier = shifted(precond, "tm", 1)
    disp_rim = padded_2(precond[0:1], (("rows", 1),), 1)
    laplace = neighbours(disp_rim)[0] - 4.0 * precond[0]
    first = precond[0] - earlier[0] - precond[1]
    second = precond[1] - earlier[1] - coupling * laplace
    image = jnp.stack([first, second])
    inner = jnp.sum(basis[:, :, 0] * image[None], axis=(1, 2, 3))
    count = 2.0 * steps * rows_dev * lax.axis_size("rows") * cols
    squares = jnp.sum(image * image) / count
    local_terms = jnp.concatenate([inner, squares[None]])
    gram = lax.psum(local_terms, ("tm", "rows"))
    return (precond[:, None], image[:, None], gram)


def solution(mesh):
    in_specs = (P(None, "tm", "rows", None), P(None, None, "tm", "rows", None))
    out_specs = (P(None, "tm", "rows", None), P(None, "tm", "rows", None), P())
    return jax.shard_map(
        on_device, mesh=mesh, in_specs=in_specs, out_specs=out_specs, check_vma=False
    )
```

profile of v0, /device:TPU:0, one launch (start us, length us, event | category | flops | bytes accessed | tf_op | source)
XLA Modules:
  0.0 169.4 jit_solution(10434036143663607024)
XLA Ops:
  2.6 19.4 %reduce.4 = f32[4096,2]{1,0:T(8,128)} reduce(f32[4096,1,2]{2,1,0:T(1,128)S(1)} %bitcast.83, f32[]{:T(128)} %broadcast.139), dimensions={1}, to_apply=%bitcast.65.reduce_sub_computation | reduce | bytes 65540
  22.0 3.0 %reshape.138 = f32[16,1,512]{2,1,0:T(1,128)S(1)} reshape(f32[4096,2]{1,0:T(8,128)} %reduce.4) | data formatting | bytes 65536
  25.0 15.5 %all_to_all.63 = f32[16,1,512]{2,1,0:T(1,128)S(1)} all-to-all(f32[16,1,512]{2,1,0:T(1,128)S(1)} %reshape.138), channel_id=1, replica_groups=mesh['tm'=16,'rows'=2] {'tm'}, dimensions={0} | all-to-all | bytes 65536 | tf_op jit(solution)/shard_map/all_to_all | solution.py:61
  41.3 3.4 %reshape.139 = f32[4096,1,2]{2,1,0:T(1,128)S(1)} reshape(f32[16,512]{1,0:T(8,128)S(1)} %reduce.5) | data formatting | bytes 65536
  46.5 3.5 %all-to-all-start.1 = ((f32[16,2,2,256]{3,2,1,0:T(2,128)}), f32[16,2,2,256]{3,2,1,0:T(2,128)S(1)}, u32[]{:S(2)}, u32[]{:S(2)}) async-start(f32[16,2,2,256]{3,2,1,0:T(2,128)} %copy.48), calls=%async_computation.1 | async-start | bytes 131072 | tf_op jit(solution)/shard_map/all_to_all | solution.py:68
  50.2 7.2 %all-to-all-done.1 = f32[16,2,2,256]{3,2,1,0:T(2,128)S(1)} async-done(((f32[16,2,2,256]{3,2,1,0:T(2,128)}), f32[16,2,2,256]{3,2,1,0:T(2,128)S(1)}, u32[]{:S(2)}, u32[]{:S(2)}) %all-to-all-start.1) | async-done | bytes 65568 | tf_op jit(solution)/shard_map/all_to_all | solution.py:68
  57.6 1.3 collective-permute-start
  58.9 3.0 %collective-permute-start.1 = (f32[2,1,512]{2,1,0:T(1,128)S(1)}, f32[2,1,512]{2,1,0:T(1,128)S(1)}, u32[]{:S(2)}, u32[]{:S(2)}) collective-permute-start(f32[2,1,512]{2,1,0:T(1,128)S(1)} %get-tuple-element.26), channel_id=1, source_target_pairs={{0,1},{2,3},{4,5},{6,7},{8,9},{10,11},{12,13},{14,15},{16,17},{18,... | collective-permute-start | bytes 12296 | tf_op jit(solution)/shard_map/ppermute | solution.py:18
  62.9 1.3 collective-permute-start.2
  64.2 3.0 %collective-permute-start.3 = (f32[2,1,512]{2,1,0:T(1,128)S(1)}, f32[2,1,512]{2,1,0:T(1,128)S(1)}, u32[]{:S(2)}, u32[]{:S(2)}) collective-permute-start(f32[2,1,512]{2,1,0:T(1,128)S(1)} %get-tuple-element.22), channel_id=1, source_target_pairs={{0,1},{2,3},{4,5},{6,7},{8,9},{10,11},{12,13},{14,15},{16,17},{18,... | collective-permute-start | bytes 12296 | tf_op jit(solution)/shard_map/ppermute | solution.py:18
  68.1 1.3 collective-permute-start.4
  69.4 3.2 %collective-permute-start.5 = (f32[2,1,512]{2,1,0:T(1,128)S(1)}, f32[2,1,512]{2,1,0:T(1,128)S(1)}, u32[]{:S(2)}, u32[]{:S(2)}) collective-permute-start(f32[2,1,512]{2,1,0:T(1,128)S(1)} %get-tuple-element.18), channel_id=1, source_target_pairs={{0,1},{2,3},{4,5},{6,7},{8,9},{10,11},{12,13},{14,15},{16,17},{18,... | collective-permute-start | bytes 12296 | tf_op jit(solution)/shard_map/ppermute | solution.py:18
  73.5 4.4 %copy.51 = f32[1,2,2,4096]{2,1,0,3:T(2,128)} copy(f32[1,2,2,4096]{3,1,2,0:T(2,128)S(1)} %pad_maximum_fusion.1) | data formatting | bytes 131072 | tf_op jit(solution)/shard_map/stack | solution.py:86
  77.9 8.1 %reshape.140 = f32[16,1,1024]{2,1,0:T(1,128)} reshape(f32[4096,1,2,2]{3,2,1,0:T(2,128)} %bitcast.81) | data formatting | bytes 131072
  86.0 3.5 %all-to-all-start.2 = ((f32[16,1,1024]{2,1,0:T(1,128)}), f32[16,1,1024]{2,1,0:T(1,128)S(1)}, u32[]{:S(2)}, u32[]{:S(2)}) async-start(f32[16,1,1024]{2,1,0:T(1,128)} %reshape.140), calls=%async_computation.2 | async-start | bytes 131072 | tf_op jit(solution)/shard_map/all_to_all | solution.py:87
  89.5 7.5 %all-to-all-done.2 = f32[16,1,1024]{2,1,0:T(1,128)S(1)} async-done(((f32[16,1,1024]{2,1,0:T(1,128)}), f32[16,1,1024]{2,1,0:T(1,128)S(1)}, u32[]{:S(2)}, u32[]{:S(2)}) %all-to-all-start.2) | async-done | bytes 65568 | tf_op jit(solution)/shard_map/all_to_all | solution.py:87
  97.8 7.7 %reshape.141 = f32[4096,1,2,2]{3,2,1,0:T(2,128)} reshape(f32[16,1024]{1,0:T(8,128)S(1)} %reduce.6) | data formatting | bytes 131072
  105.6 3.6 %copy.57 = f32[1,2,2,16,256]{4,3,2,1,0:T(8,128)S(1)} copy(f32[1,2,2,16,256]{2,1,4,3,0:T(2,128)} %bitcast.82) | data formatting | bytes 131072 | tf_op jit(solution)/shard_map/all_to_all | solution.py:87
  109.7 10.0 %all_to_all.64 = f32[16,2,256]{2,1,0:T(2,128)S(1)} all-to-all(f32[16,2,256]{2,1,0:T(2,128)S(1)} %reshape.134), channel_id=1, replica_groups=mesh['tm'=16,'rows'=2] {'tm'}, dimensions={0} | all-to-all | bytes 65536 | tf_op jit(solution)/shard_map/all_to_all | solution.py:97
  119.8 2.6 %collective-permute-start.6 = (f32[2,8,512]{2,1,0:T(8,128)S(1)}, f32[2,8,512]{2,1,0:T(8,128)S(1)}, u32[]{:S(2)}, u32[]{:S(2)}) collective-permute-start(f32[2,8,512]{2,1,0:T(8,128)S(1)} %reshape_squeeze.15), channel_id=1, source_target_pairs={{0,2},{2,4},{4,6},{6,8},{8,10},{10,12},{12,14},{14,16},{16,18},{18... | collective-permute-start | bytes 98312 | tf_op jit(solution)/shard_map/ppermute | solution.py:27
  122.4 1.3 collective-permute-start.7
  123.7 3.0 %collective-permute-start.8 = (f32[1,1,512]{2,1,0:T(1,128)S(1)}, f32[1,1,512]{2,1,0:T(1,128)S(1)}, u32[]{:S(2)}, u32[]{:S(2)}) collective-permute-start(f32[1,1,512]{2,1,0:T(1,128)S(1)} %get-tuple-element.30), channel_id=1, source_target_pairs={{0,1},{2,3},{4,5},{6,7},{8,9},{10,11},{12,13},{14,15},{16,17},{18,... | collective-permute-start | bytes 6152 | tf_op jit(solution)/shard_map/ppermute | solution.py:18
  127.7 1.2 pad_maximum_fusion.18
  130.4 39.0 %psum.7 = f32[5]{0:T(128)} all-reduce(f32[5]{0:T(128)S(1)} %pad_maximum_fusion.21), channel_id=1, replica_groups=mesh['tm'=16,'rows'=2] {'tm','rows'}, use_global_device_ids=true, to_apply=%region_2.3 | all-reduce | flops 5 | bytes 40 | tf_op jit(solution)/shard_map/psum | solution.py:109
  (66 shorter events, 10.2 us)
Async XLA Ops:
  46.5 11.0 %all-to-all-start.1 = ((f32[16,2,2,256]{3,2,1,0:T(2,128)}), f32[16,2,2,256]{3,2,1,0:T(2,128)S(1)}, u32[]{:S(2)}, u32[]{:S(2)}) async-start(f32[16,2,2,256]{3,2,1,0:T(2,128)} %copy.48), calls=%async_computation.1 | async-start | bytes 131072 | tf_op jit(solution)/shard_map/all_to_all | solution.py:68
  57.6 4.3 %collective-permute-start = (f32[2,1,512]{2,1,0:T(1,128)S(1)}, f32[2,1,512]{2,1,0:T(1,128)S(1)}, u32[]{:S(2)}, u32[]{:S(2)}) collective-permute-start(f32[2,1,512]{2,1,0:T(1,128)S(1)} %get-tuple-element.25), channel_id=1, source_target_pairs={{1,0},{3,2},{5,4},{7,6},{9,8},{11,10},{13,12},{15,14},{17,16},{19,... | collective-permute-start | bytes 12296 | tf_op jit(solution)/shard_map/ppermute | solution.py:19
  58.9 3.8 %collective-permute-start.1 = (f32[2,1,512]{2,1,0:T(1,128)S(1)}, f32[2,1,512]{2,1,0:T(1,128)S(1)}, u32[]{:S(2)}, u32[]{:S(2)}) collective-permute-start(f32[2,1,512]{2,1,0:T(1,128)S(1)} %get-tuple-element.26), channel_id=1, source_target_pairs={{0,1},{2,3},{4,5},{6,7},{8,9},{10,11},{12,13},{14,15},{16,17},{18,... | collective-permute-start | bytes 12296 | tf_op jit(solution)/shard_map/ppermute | solution.py:18
  62.9 4.3 %collective-permute-start.2 = (f32[2,1,512]{2,1,0:T(1,128)S(1)}, f32[2,1,512]{2,1,0:T(1,128)S(1)}, u32[]{:S(2)}, u32[]{:S(2)}) collective-permute-start(f32[2,1,512]{2,1,0:T(1,128)S(1)} %get-tuple-element.21), channel_id=1, source_target_pairs={{1,0},{3,2},{5,4},{7,6},{9,8},{11,10},{13,12},{15,14},{17,16},{19,... | collective-permute-start | bytes 12296 | tf_op jit(solution)/shard_map/ppermute | solution.py:19
  64.2 3.8 %collective-permute-start.3 = (f32[2,1,512]{2,1,0:T(1,128)S(1)}, f32[2,1,512]{2,1,0:T(1,128)S(1)}, u32[]{:S(2)}, u32[]{:S(2)}) collective-permute-start(f32[2,1,512]{2,1,0:T(1,128)S(1)} %get-tuple-element.22), channel_id=1, source_target_pairs={{0,1},{2,3},{4,5},{6,7},{8,9},{10,11},{12,13},{14,15},{16,17},{18,... | collective-permute-start | bytes 12296 | tf_op jit(solution)/shard_map/ppermute | solution.py:18
  68.1 4.5 %collective-permute-start.4 = (f32[2,1,512]{2,1,0:T(1,128)S(1)}, f32[2,1,512]{2,1,0:T(1,128)S(1)}, u32[]{:S(2)}, u32[]{:S(2)}) collective-permute-start(f32[2,1,512]{2,1,0:T(1,128)S(1)} %get-tuple-element.17), channel_id=1, source_target_pairs={{1,0},{3,2},{5,4},{7,6},{9,8},{11,10},{13,12},{15,14},{17,16},{19,... | collective-permute-start | bytes 12296 | tf_op jit(solution)/shard_map/ppermute | solution.py:19
  69.4 3.8 %collective-permute-start.5 = (f32[2,1,512]{2,1,0:T(1,128)S(1)}, f32[2,1,512]{2,1,0:T(1,128)S(1)}, u32[]{:S(2)}, u32[]{:S(2)}) collective-permute-start(f32[2,1,512]{2,1,0:T(1,128)S(1)} %get-tuple-element.18), channel_id=1, source_target_pairs={{0,1},{2,3},{4,5},{6,7},{8,9},{10,11},{12,13},{14,15},{16,17},{18,... | collective-permute-start | bytes 12296 | tf_op jit(solution)/shard_map/ppermute | solution.py:18
  86.0 11.0 %all-to-all-start.2 = ((f32[16,1,1024]{2,1,0:T(1,128)}), f32[16,1,1024]{2,1,0:T(1,128)S(1)}, u32[]{:S(2)}, u32[]{:S(2)}) async-start(f32[16,1,1024]{2,1,0:T(1,128)} %reshape.140), calls=%async_computation.2 | async-start | bytes 131072 | tf_op jit(solution)/shard_map/all_to_all | solution.py:87
  105.6 24.0 %copy-start = (f32[4,2,1,8,512]{4,3,2,1,0:T(8,128)S(1)}, f32[4,2,1,8,512]{4,3,2,1,0:T(8,128)}, u32[]{:S(2)}) copy-start(f32[4,2,1,8,512]{4,3,2,1,0:T(8,128)} %param.3) | copy-start | bytes 393220
  119.8 7.8 %collective-permute-start.6 = (f32[2,8,512]{2,1,0:T(8,128)S(1)}, f32[2,8,512]{2,1,0:T(8,128)S(1)}, u32[]{:S(2)}, u32[]{:S(2)}) collective-permute-start(f32[2,8,512]{2,1,0:T(8,128)S(1)} %reshape_squeeze.15), channel_id=1, source_target_pairs={{0,2},{2,4},{4,6},{6,8},{8,10},{10,12},{12,14},{14,16},{16,18},{18... | collective-permute-start | bytes 98312 | tf_op jit(solution)/shard_map/ppermute | solution.py:27
  122.4 4.4 %collective-permute-start.7 = (f32[1,1,512]{2,1,0:T(1,128)S(1)}, f32[1,1,512]{2,1,0:T(1,128)S(1)}, u32[]{:S(2)}, u32[]{:S(2)}) collective-permute-start(f32[1,1,512]{2,1,0:T(1,128)S(1)} %get-tuple-element.29), channel_id=1, source_target_pairs={{1,0},{3,2},{5,4},{7,6},{9,8},{11,10},{13,12},{15,14},{17,16},{19,... | collective-permute-start | bytes 6152 | tf_op jit(solution)/shard_map/ppermute | solution.py:19
  123.7 3.8 %collective-permute-start.8 = (f32[1,1,512]{2,1,0:T(1,128)S(1)}, f32[1,1,512]{2,1,0:T(1,128)S(1)}, u32[]{:S(2)}, u32[]{:S(2)}) collective-permute-start(f32[1,1,512]{2,1,0:T(1,128)S(1)} %get-tuple-element.30), channel_id=1, source_target_pairs={{0,1},{2,3},{4,5},{6,7},{8,9},{10,11},{12,13},{14,15},{16,17},{18,... | collective-permute-start | bytes 6152 | tf_op jit(solution)/shard_map/ppermute | solution.py:18
where the time goes:
time: 170 us; the launch traced here: 169 us
  blocking collectives  64.5 us (38%)
  local copies, waits for them, and re-layouts  33.7 us (20%)
  starting transfers between devices  27 us (16%)
  other arithmetic  23.6 us (14%)
  waiting for transfers between devices  17.7 us (10%)
  between operations  2.06 us (1%)
    psum x1, blocking collectives, on_device(): gram = lax.psum(local_terms, ('tm', 'rows'))  39 us
    unnamed x10, local copies, waits for them, and re-layouts  22.8 us
    unnamed x1, other arithmetic  19.4 us
    all_to_all x1, blocking collectives, on_device(): lax.all_to_all(scaled.reshape(1, 2, cells), 'tm', split_axis=2, concat_ax...  15.5 us
    ppermute x4, starting transfers between devices, padded_2(): before = lax.ppermute(last, axis, up)  12.3 us
    all_to_all x1, blocking collectives, on_device(): lax.all_to_all(history, 'tm', split_axis=0, concat_axis=2, tiled=True)  9.98 us
    all_to_all x1, waiting for transfers between devices, on_device(): lax.all_to_all(yhat.reshape(1, 2, 2, cells), 'tm', split_axis=3, concat_a...  7.49 us
    all_to_all x1, waiting for transfers between devices, on_device(): lax.all_to_all(stacked, 'tm', split_axis=0, concat_axis=3, tiled=True)  7.25 us
  transfers between devices with their start and end apart: 11, of which 6 were waited for; matrix products, arithmetic and copies ran while one was open for 0% of the time, Pallas kernels for 0%

commit v1 on v0

--- a/solution.py
+++ b/solution.py
@@ -6,6 +6,12 @@
 
 SWEEPS = 4
 ALPHA = 0.01
+
+
+def summed_here(value, mesh_axis):
+    parts = lax.all_gather(value, mesh_axis, axis=0, tiled=False)
+    total = parts.sum(axis=0)
+    return total
 
 
 def padded_2(shard, sides, width):
@@ -106,7 +112,7 @@
     count = 2.0 * steps * rows_dev * lax.axis_size("rows") * cols
     squares = jnp.sum(image * image) / count
     local_terms = jnp.concatenate([inner, squares[None]])
-    gram = lax.psum(local_terms, ("tm", "rows"))
+    gram = summed_here(local_terms, ("tm", "rows"))
     return (precond[:, None], image[:, None], gram)
 
 

time: 170 us -> 170 us (level)
    unnamed x0 -> x1, blocking collectives: none -> 39 us
    psum x1 -> x0, blocking collectives: 39 us -> none  [on_device(): gram = lax.psum(local_terms, ('tm', 'rows'))]
    unnamed x1 -> x2, other arithmetic: 19.4 us -> 19.5 us
    unnamed x10 -> x11, local copies, waits for them, and re-layouts: 22.8 us -> 22.8 us
where the time goes in v1:
time: 170 us
  blocking collectives  64.6 us (38%)
  local copies, waits for them, and re-layouts  33.8 us (20%)
  starting transfers between devices  27 us (16%)
  other arithmetic  24.2 us (14%)
  waiting for transfers between devices  17.1 us (10%)
  between operations  2.02 us (1%)
    unnamed x1, blocking collectives  39 us
    unnamed x11, local copies, waits for them, and re-layouts  22.8 us
    unnamed x2, other arithmetic  19.5 us
    all_to_all x1, blocking collectives, on_device(): lax.all_to_all(scaled.reshape(1, 2, cells), 'tm', split_axis=2, concat_ax...  15.5 us
    ppermute x4, starting transfers between devices, padded_2(): before = lax.ppermute(last, axis, up)  12.3 us
    all_to_all x1, blocking collectives, on_device(): lax.all_to_all(history, 'tm', split_axis=0, concat_axis=2, tiled=True)  9.98 us
    all_to_all x1, waiting for transfers between devices, on_device(): lax.all_to_all(yhat.reshape(1, 2, 2, cells), 'tm', split_axis=3, concat_a...  7.49 us
    all_to_all x1, waiting for transfers between devices, on_device(): lax.all_to_all(stacked, 'tm', split_axis=0, concat_axis=3, tiled=True)  7.25 us
  transfers between devices with their start and end apart: 11, of which 6 were waited for; matrix products, arithmetic and copies ran while one was open for 0% of the time, Pallas kernels for 0%

profile of v1, /device:TPU:0, one launch (start us, length us, event | category | flops | bytes accessed | tf_op | source)
XLA Modules:
  0.0 169.5 jit_solution(8464165860491672188)
XLA Ops:
  2.6 19.4 %reduce.4 = f32[4096,2]{1,0:T(8,128)} reduce(f32[4096,1,2]{2,1,0:T(1,128)S(1)} %bitcast.83, f32[]{:T(128)} %broadcast.140), dimensions={1}, to_apply=%bitcast.65.reduce_sub_computation | reduce | bytes 65540
  22.0 3.0 %reshape.141 = f32[16,1,512]{2,1,0:T(1,128)S(1)} reshape(f32[4096,2]{1,0:T(8,128)} %reduce.4) | data formatting | bytes 65536
  25.0 15.5 %all_to_all.63 = f32[16,1,512]{2,1,0:T(1,128)S(1)} all-to-all(f32[16,1,512]{2,1,0:T(1,128)S(1)} %reshape.141), channel_id=1, replica_groups=mesh['tm'=16,'rows'=2] {'tm'}, dimensions={0} | all-to-all | bytes 65536 | tf_op jit(solution)/shard_map/all_to_all | solution.py:67
  41.3 3.4 %reshape.142 = f32[4096,1,2]{2,1,0:T(1,128)S(1)} reshape(f32[16,512]{1,0:T(8,128)S(1)} %reduce.5) | data formatting | bytes 65536
  46.5 3.5 %all-to-all-start.1 = ((f32[16,2,2,256]{3,2,1,0:T(2,128)}), f32[16,2,2,256]{3,2,1,0:T(2,128)S(1)}, u32[]{:S(2)}, u32[]{:S(2)}) async-start(f32[16,2,2,256]{3,2,1,0:T(2,128)} %copy.48), calls=%async_computation.1 | async-start | bytes 131072 | tf_op jit(solution)/shard_map/all_to_all | solution.py:74
  50.3 7.2 %all-to-all-done.1 = f32[16,2,2,256]{3,2,1,0:T(2,128)S(1)} async-done(((f32[16,2,2,256]{3,2,1,0:T(2,128)}), f32[16,2,2,256]{3,2,1,0:T(2,128)S(1)}, u32[]{:S(2)}, u32[]{:S(2)}) %all-to-all-start.1) | async-done | bytes 65568 | tf_op jit(solution)/shard_map/all_to_all | solution.py:74
  57.6 1.3 collective-permute-start
  58.9 3.0 %collective-permute-start.1 = (f32[2,1,512]{2,1,0:T(1,128)S(1)}, f32[2,1,512]{2,1,0:T(1,128)S(1)}, u32[]{:S(2)}, u32[]{:S(2)}) collective-permute-start(f32[2,1,512]{2,1,0:T(1,128)S(1)} %get-tuple-element.26), channel_id=1, source_target_pairs={{0,1},{2,3},{4,5},{6,7},{8,9},{10,11},{12,13},{14,15},{16,17},{18,... | collective-permute-start | bytes 12296 | tf_op jit(solution)/shard_map/ppermute | solution.py:24
  62.9 1.3 collective-permute-start.2
  64.2 3.0 %collective-permute-start.3 = (f32[2,1,512]{2,1,0:T(1,128)S(1)}, f32[2,1,512]{2,1,0:T(1,128)S(1)}, u32[]{:S(2)}, u32[]{:S(2)}) collective-permute-start(f32[2,1,512]{2,1,0:T(1,128)S(1)} %get-tuple-element.22), channel_id=1, source_target_pairs={{0,1},{2,3},{4,5},{6,7},{8,9},{10,11},{12,13},{14,15},{16,17},{18,... | collective-permute-start | bytes 12296 | tf_op jit(solution)/shard_map/ppermute | solution.py:24
  68.1 1.3 collective-permute-start.4
  69.4 3.2 %collective-permute-start.5 = (f32[2,1,512]{2,1,0:T(1,128)S(1)}, f32[2,1,512]{2,1,0:T(1,128)S(1)}, u32[]{:S(2)}, u32[]{:S(2)}) collective-permute-start(f32[2,1,512]{2,1,0:T(1,128)S(1)} %get-tuple-element.18), channel_id=1, source_target_pairs={{0,1},{2,3},{4,5},{6,7},{8,9},{10,11},{12,13},{14,15},{16,17},{18,... | collective-permute-start | bytes 12296 | tf_op jit(solution)/shard_map/ppermute | solution.py:24
  73.5 4.4 %copy.51 = f32[1,2,2,4096]{2,1,0,3:T(2,128)} copy(f32[1,2,2,4096]{3,1,2,0:T(2,128)S(1)} %pad_maximum_fusion.1) | data formatting | bytes 131072 | tf_op jit(solution)/shard_map/stack | solution.py:92
  77.9 8.1 %reshape.143 = f32[16,1,1024]{2,1,0:T(1,128)} reshape(f32[4096,1,2,2]{3,2,1,0:T(2,128)} %bitcast.81) | data formatting | bytes 131072
  86.0 3.5 %all-to-all-start.2 = ((f32[16,1,1024]{2,1,0:T(1,128)}), f32[16,1,1024]{2,1,0:T(1,128)S(1)}, u32[]{:S(2)}, u32[]{:S(2)}) async-start(f32[16,1,1024]{2,1,0:T(1,128)} %reshape.143), calls=%async_computation.2 | async-start | bytes 131072 | tf_op jit(solution)/shard_map/all_to_all | solution.py:93
  89.5 7.5 %all-to-all-done.2 = f32[16,1,1024]{2,1,0:T(1,128)S(1)} async-done(((f32[16,1,1024]{2,1,0:T(1,128)}), f32[16,1,1024]{2,1,0:T(1,128)S(1)}, u32[]{:S(2)}, u32[]{:S(2)}) %all-to-all-start.2) | async-done | bytes 65568 | tf_op jit(solution)/shard_map/all_to_all | solution.py:93
  97.8 7.7 %reshape.144 = f32[4096,1,2,2]{3,2,1,0:T(2,128)} reshape(f32[16,1024]{1,0:T(8,128)S(1)} %reduce.6) | data formatting | bytes 131072
  105.6 3.6 %copy.57 = f32[1,2,2,16,256]{4,3,2,1,0:T(8,128)S(1)} copy(f32[1,2,2,16,256]{2,1,4,3,0:T(2,128)} %bitcast.82) | data formatting | bytes 131072 | tf_op jit(solution)/shard_map/all_to_all | solution.py:93
  109.7 10.0 %all_to_all.64 = f32[16,2,256]{2,1,0:T(2,128)S(1)} all-to-all(f32[16,2,256]{2,1,0:T(2,128)S(1)} %reshape.134), channel_id=1, replica_groups=mesh['tm'=16,'rows'=2] {'tm'}, dimensions={0} | all-to-all | bytes 65536 | tf_op jit(solution)/shard_map/all_to_all | solution.py:103
  119.8 2.6 %collective-permute-start.6 = (f32[2,8,512]{2,1,0:T(8,128)S(1)}, f32[2,8,512]{2,1,0:T(8,128)S(1)}, u32[]{:S(2)}, u32[]{:S(2)}) collective-permute-start(f32[2,8,512]{2,1,0:T(8,128)S(1)} %reshape_squeeze.15), channel_id=1, source_target_pairs={{0,2},{2,4},{4,6},{6,8},{8,10},{10,12},{12,14},{14,16},{16,18},{18... | collective-permute-start | bytes 98312 | tf_op jit(solution)/shard_map/ppermute | solution.py:33
  122.5 1.3 collective-permute-start.7
  123.8 3.0 %collective-permute-start.8 = (f32[1,1,512]{2,1,0:T(1,128)S(1)}, f32[1,1,512]{2,1,0:T(1,128)S(1)}, u32[]{:S(2)}, u32[]{:S(2)}) collective-permute-start(f32[1,1,512]{2,1,0:T(1,128)S(1)} %get-tuple-element.30), channel_id=1, source_target_pairs={{0,1},{2,3},{4,5},{6,7},{8,9},{10,11},{12,13},{14,15},{16,17},{18,... | collective-permute-start | bytes 6152 | tf_op jit(solution)/shard_map/ppermute | solution.py:24
  127.7 1.2 pad_maximum_fusion.18
  129.9 39.0 %all-reduce.4 = f32[160]{0:T(256)S(1)} all-reduce(f32[160]{0:T(256)S(1)} %maximum_dynamic-update-slice_fusion), channel_id=2, replica_groups=mesh['tm'=16,'rows'=2] {'tm','rows'}, use_global_device_ids=true, to_apply=%add.4 | all-reduce | flops 160 | bytes 1280
  (69 shorter events, 10.3 us)
Async XLA Ops:
  46.5 11.0 %all-to-all-start.1 = ((f32[16,2,2,256]{3,2,1,0:T(2,128)}), f32[16,2,2,256]{3,2,1,0:T(2,128)S(1)}, u32[]{:S(2)}, u32[]{:S(2)}) async-start(f32[16,2,2,256]{3,2,1,0:T(2,128)} %copy.48), calls=%async_computation.1 | async-start | bytes 131072 | tf_op jit(solution)/shard_map/all_to_all | solution.py:74
  57.6 4.3 %collective-permute-start = (f32[2,1,512]{2,1,0:T(1,128)S(1)}, f32[2,1,512]{2,1,0:T(1,128)S(1)}, u32[]{:S(2)}, u32[]{:S(2)}) collective-permute-start(f32[2,1,512]{2,1,0:T(1,128)S(1)} %get-tuple-element.25), channel_id=1, source_target_pairs={{1,0},{3,2},{5,4},{7,6},{9,8},{11,10},{13,12},{15,14},{17,16},{19,... | collective-permute-start | bytes 12296 | tf_op jit(solution)/shard_map/ppermute | solution.py:25
  58.9 3.8 %collective-permute-start.1 = (f32[2,1,512]{2,1,0:T(1,128)S(1)}, f32[2,1,512]{2,1,0:T(1,128)S(1)}, u32[]{:S(2)}, u32[]{:S(2)}) collective-permute-start(f32[2,1,512]{2,1,0:T(1,128)S(1)} %get-tuple-element.26), channel_id=1, source_target_pairs={{0,1},{2,3},{4,5},{6,7},{8,9},{10,11},{12,13},{14,15},{16,17},{18,... | collective-permute-start | bytes 12296 | tf_op jit(solution)/shard_map/ppermute | solution.py:24
  62.9 4.3 %collective-permute-start.2 = (f32[2,1,512]{2,1,0:T(1,128)S(1)}, f32[2,1,512]{2,1,0:T(1,128)S(1)}, u32[]{:S(2)}, u32[]{:S(2)}) collective-permute-start(f32[2,1,512]{2,1,0:T(1,128)S(1)} %get-tuple-element.21), channel_id=1, source_target_pairs={{1,0},{3,2},{5,4},{7,6},{9,8},{11,10},{13,12},{15,14},{17,16},{19,... | collective-permute-start | bytes 12296 | tf_op jit(solution)/shard_map/ppermute | solution.py:25
  64.2 3.8 %collective-permute-start.3 = (f32[2,1,512]{2,1,0:T(1,128)S(1)}, f32[2,1,512]{2,1,0:T(1,128)S(1)}, u32[]{:S(2)}, u32[]{:S(2)}) collective-permute-start(f32[2,1,512]{2,1,0:T(1,128)S(1)} %get-tuple-element.22), channel_id=1, source_target_pairs={{0,1},{2,3},{4,5},{6,7},{8,9},{10,11},{12,13},{14,15},{16,17},{18,... | collective-permute-start | bytes 12296 | tf_op jit(solution)/shard_map/ppermute | solution.py:24
  68.1 4.5 %collective-permute-start.4 = (f32[2,1,512]{2,1,0:T(1,128)S(1)}, f32[2,1,512]{2,1,0:T(1,128)S(1)}, u32[]{:S(2)}, u32[]{:S(2)}) collective-permute-start(f32[2,1,512]{2,1,0:T(1,128)S(1)} %get-tuple-element.17), channel_id=1, source_target_pairs={{1,0},{3,2},{5,4},{7,6},{9,8},{11,10},{13,12},{15,14},{17,16},{19,... | collective-permute-start | bytes 12296 | tf_op jit(solution)/shard_map/ppermute | solution.py:25
  69.4 3.8 %collective-permute-start.5 = (f32[2,1,512]{2,1,0:T(1,128)S(1)}, f32[2,1,512]{2,1,0:T(1,128)S(1)}, u32[]{:S(2)}, u32[]{:S(2)}) collective-permute-start(f32[2,1,512]{2,1,0:T(1,128)S(1)} %get-tuple-element.18), channel_id=1, source_target_pairs={{0,1},{2,3},{4,5},{6,7},{8,9},{10,11},{12,13},{14,15},{16,17},{18,... | collective-permute-start | bytes 12296 | tf_op jit(solution)/shard_map/ppermute | solution.py:24
  86.0 11.0 %all-to-all-start.2 = ((f32[16,1,1024]{2,1,0:T(1,128)}), f32[16,1,1024]{2,1,0:T(1,128)S(1)}, u32[]{:S(2)}, u32[]{:S(2)}) async-start(f32[16,1,1024]{2,1,0:T(1,128)} %reshape.143), calls=%async_computation.2 | async-start | bytes 131072 | tf_op jit(solution)/shard_map/all_to_all | solution.py:93
  105.6 24.0 %copy-start = (f32[4,2,1,8,512]{4,3,2,1,0:T(8,128)S(1)}, f32[4,2,1,8,512]{4,3,2,1,0:T(8,128)}, u32[]{:S(2)}) copy-start(f32[4,2,1,8,512]{4,3,2,1,0:T(8,128)} %param.3) | copy-start | bytes 393220
  119.8 7.8 %collective-permute-start.6 = (f32[2,8,512]{2,1,0:T(8,128)S(1)}, f32[2,8,512]{2,1,0:T(8,128)S(1)}, u32[]{:S(2)}, u32[]{:S(2)}) collective-permute-start(f32[2,8,512]{2,1,0:T(8,128)S(1)} %reshape_squeeze.15), channel_id=1, source_target_pairs={{0,2},{2,4},{4,6},{6,8},{8,10},{10,12},{12,14},{14,16},{16,18},{18... | collective-permute-start | bytes 98312 | tf_op jit(solution)/shard_map/ppermute | solution.py:33
  122.5 5.0 %collective-permute-start.7 = (f32[1,1,512]{2,1,0:T(1,128)S(1)}, f32[1,1,512]{2,1,0:T(1,128)S(1)}, u32[]{:S(2)}, u32[]{:S(2)}) collective-permute-start(f32[1,1,512]{2,1,0:T(1,128)S(1)} %get-tuple-element.29), channel_id=1, source_target_pairs={{1,0},{3,2},{5,4},{7,6},{9,8},{11,10},{13,12},{15,14},{17,16},{19,... | collective-permute-start | bytes 6152 | tf_op jit(solution)/shard_map/ppermute | solution.py:25
  123.8 3.8 %collective-permute-start.8 = (f32[1,1,512]{2,1,0:T(1,128)S(1)}, f32[1,1,512]{2,1,0:T(1,128)S(1)}, u32[]{:S(2)}, u32[]{:S(2)}) collective-permute-start(f32[1,1,512]{2,1,0:T(1,128)S(1)} %get-tuple-element.30), channel_id=1, source_target_pairs={{0,1},{2,3},{4,5},{6,7},{8,9},{10,11},{12,13},{14,15},{16,17},{18,... | collective-permute-start | bytes 6152 | tf_op jit(solution)/shard_map/ppermute | solution.py:24
